TPU v7x, 32 devices: a whole 2x2x4 slice. The times are simulated.
32 devices in a mesh: groups: 2 (over y), tok: 8 (over z, core), head: 2 (over x), pair: 1.
Axes of the slice: x: 2, y: 2, z: 4, core: 2. Of those that a mesh axis runs over, the one named last changes fastest.
Arguments:
- queries: bfloat16 [2048, 4096], P(('groups', 'tok'), ('head', 'pair')), parts along dimension 0, may hold values from -6 to 6
- keys_values: bfloat16 [2048, 1024], P(('groups', 'tok'), ('head', 'pair')), parts along dimension 0, may hold values from -6 to 6
- sink_logits: float32 [64], P(('head', 'pair')), may hold values from -2 to 3
- residual: bfloat16 [2048, 2880], P(('groups', 'tok')), parts along dimension 0, may hold values from -60 to 60
- out_weight: bfloat16 [4096, 2880], P(('head', 'pair')), may hold values from -0.09375 to 0.09375
- norm_gain: float32 [2880], replicated, may hold values from 0.5 to 1.5
- expert_ids: int32 [2048, 4], P(('groups', 'tok')), parts along dimension 0, may hold values from 0 to 7, all different within a row; in each aligned block of 128 rows (0 to 127, 128 to 255, ...) at most 80 rows name the same one
- route_weights: float32 [2048, 4], P(('groups', 'tok')), parts along dimension 0, may hold values from 0.1 to 1
- gate_up: bfloat16 [8, 2880, 2, 1440], P('tok', None, None, ('head', 'pair')), may hold values from -0.109375 to 0.109375
- down_weight: bfloat16 [8, 1440, 2880], P('tok', ('head', 'pair')), may hold values from -0.21875 to 0.21875
Outputs:
- layer_output: bfloat16 [2048, 2880], P(('groups', 'tok'), ('head', 'pair')), parts along dimension 0
There are 2 independent parts, one for each index of `groups`. A program takes and returns all parts, laid end to end along the dimension named above; an argument that names none is the same for every part. Nothing has to cross between parts.
Inputs may be any that keep to these rules, and one draw needn't show every extreme that they name: `expert_ids`: in each aligned block of 128 rows (the rows of one index of tok), a row names 4 different experts and no expert is named by more than 80 rows.
All inputs are finite; a program needn't handle non-finite values.
Results may differ from a plain program's by a relative error of at most 0.01.
Values may be sent and summed in bfloat16 or wider, within the bound.
A program may use at most 128 MiB of HBM per device.

v0:
```python
import jax
import jax.numpy as jnp
from jax import lax
from jax.sharding import PartitionSpec as P

HEAD_DIM = 64


def slot_places(expert_ids, experts, capacity):
    tok_rows = expert_ids.shape[0]
    fanout = expert_ids.shape[1]
    flat_ids = expert_ids.reshape(-1)
    one_hot = (flat_ids[:, None] == jnp.arange(experts, dtype=jnp.int32)[None, :]).astype(jnp.int32)
    earlier = jnp.cumsum(one_hot, axis=0) - one_hot
    ranking = jnp.sum(earlier * one_hot, axis=1)
    targets = flat_ids * capacity + ranking
    sources = jnp.arange(tok_rows * fanout, dtype=jnp.int32) // fanout
    table = jnp.full((experts * capacity,), tok_rows, jnp.int32).at[targets].set(sources)
    return (targets.reshape(tok_rows, fanout), table)


def active_rows(flat_rows, gate_up):
    local_hidden = gate_up.shape[-1]
    both_columns = gate_up.reshape(flat_rows.shape[-1], 2 * local_hidden)
    both = jnp.dot(flat_rows, both_columns, preferred_element_type=jnp.float32)
    gate_part = both[:, :local_hidden]
    up_part = both[:, local_hidden:]
    return (gate_part * jax.nn.sigmoid(1.702 * gate_part) * (up_part + 1.0)).astype(jnp.bfloat16)


def per_device(
    queries,
    keys_values,
    sink_logits,
    residual,
    out_weight,
    norm_gain,
    expert_ids,
    route_weights,
    gate_up,
    down_weight,
):
    tok_rows = queries.shape[0]
    kv_groups = keys_values.shape[1] // (2 * HEAD_DIM)
    local_heads = queries.shape[1] // HEAD_DIM
    repeat = local_heads // kv_groups
    position = lax.axis_index("tok") * tok_rows + jnp.arange(tok_rows, dtype=jnp.int32)
    grouped = queries.reshape(tok_rows, kv_groups, repeat, HEAD_DIM)
    start_max = jnp.broadcast_to(
        sink_logits.reshape(kv_groups, repeat)[:, :, None], (kv_groups, repeat, tok_rows)
    )
    start_totals = jnp.ones((kv_groups, repeat, tok_rows), jnp.float32)
    start_accum = jnp.zeros((kv_groups, repeat, tok_rows, HEAD_DIM), jnp.float32)
    key_piece = lax.all_gather(keys_values, "tok", axis=0, tiled=True)
    totals = start_totals
    accum = start_accum
    count = key_piece.shape[0]
    split_piece = key_piece.reshape(count, kv_groups, 2, HEAD_DIM)
    scores = (
        jnp.einsum(
            "tgrd,ngd->grtn", grouped, split_piece[:, :, 0], preferred_element_type=jnp.float32
        )
        * 0.125
    )
    key_position = jnp.arange(count, dtype=jnp.int32)
    allowed = key_position[None, :] <= position[:, None]
    scores = jnp.where(allowed, scores, jnp.float32(-1e30))
    new_max = jnp.maximum(start_max, jnp.max(scores, axis=-1))
    decay = jnp.exp(start_max - new_max)
    weights = jnp.exp(scores - new_max[..., None])
    totals = totals * decay + jnp.sum(weights, axis=-1)
    update = jnp.einsum(
        "grtn,ngd->grtd",
        weights.astype(jnp.bfloat16),
        split_piece[:, :, 1],
        preferred_element_type=jnp.float32,
    )
    accum = accum * decay[..., None] + update
    final_max, totals, accum = (new_max, totals, accum)
    attended = (accum / totals[..., None]).astype(jnp.bfloat16)
    attended = jnp.transpose(attended, (2, 0, 1, 3)).reshape(tok_rows, local_heads * HEAD_DIM)
    width = out_weight.shape[1]
    experts = lax.axis_size("tok")
    fanout = expert_ids.shape[1]
    capacity = min(tok_rows, tok_rows * fanout * 5 // (4 * experts))
    targets, table = slot_places(expert_ids, experts, capacity)
    share = width // lax.axis_size(("head", "pair"))
    column_start = lax.axis_index(("head", "pair")) * share
    partial_value = jnp.dot(attended, out_weight, preferred_element_type=jnp.float32)
    projected = lax.psum(partial_value.astype(jnp.bfloat16), ("head", "pair")).astype(jnp.float32)
    stream = residual.astype(jnp.float32) + projected
    inverse = lax.rsqrt(jnp.mean(stream * stream, axis=-1, keepdims=True) + 1e-05)
    normed = (stream * inverse * norm_gain).astype(jnp.bfloat16)
    padded = jnp.concatenate([normed, jnp.zeros((1, width), jnp.bfloat16)], axis=0)
    outgoing = padded[table].reshape(experts, capacity, width)
    received = lax.all_to_all(outgoing, "tok", split_axis=0, concat_axis=0, tiled=True)
    shape_in = received.shape
    active = active_rows(received.reshape(-1, shape_in[-1]), gate_up)
    partial_value = jnp.dot(active, down_weight[0], preferred_element_type=jnp.float32)
    partial_out = partial_value.reshape(shape_in[:-1] + (partial_value.shape[-1],))
    stream_share = lax.dynamic_slice_in_dim(stream, column_start, share, 1)
    expert_out = lax.psum_scatter(
        partial_out.astype(jnp.bfloat16), ("head", "pair"), scatter_dimension=2, tiled=True
    )
    returned = lax.all_to_all(expert_out, "tok", split_axis=0, concat_axis=0, tiled=True)
    flat_out = returned.reshape(experts * capacity, share)
    picked = flat_out[targets]
    mixture = jnp.sum(route_weights[:, :, None] * picked.astype(jnp.float32), axis=1)
    return (stream_share + mixture).astype(jnp.bfloat16)


def solution(mesh):
    placed = (
        P(("groups", "tok"), ("head", "pair")),
        P(("groups", "tok"), ("head", "pair")),
        P(("head", "pair")),
        P(("groups", "tok"), None),
        P(("head", "pair"), None),
        P(),
        P(("groups", "tok"), None),
        P(("groups", "tok"), None),
        P("tok", None, None, ("head", "pair")),
        P("tok", ("head", "pair"), None),
    )
    return jax.shard_map(
        per_device,
        mesh=mesh,
        in_specs=placed,
        out_specs=P(("groups", "tok"), ("head", "pair")),
        check_vma=False,
    )
```

profile of v0, /device:TPU:0, one launch (start us, length us, event | category | flops | bytes accessed | tf_op | source)
XLA Modules:
  0.0 360.1 jit_solution(5080762425905200024)
XLA Ops:
  6.5 1.7 copy.27
  8.2 0.0 all-gather.2.cloned.1.call-update
  8.2 0.0 all-reduce.3.cloned.1.call-start
  8.3 0.8 copy.33
  9.1 0.1 eq.29
  9.2 0.1 eq.25
  9.3 1.3 copy.29
  10.6 0.7 broadcast_in_dim.20
  11.4 1.1 reduce-window.6
  12.5 0.2 slice_reduce_fusion
  12.8 0.1 fusion.19
  12.8 0.1 reduce_sum.44
  13.0 0.1 iota_compare_fusion
  13.1 22.5 %all-gather.2.cloned.1.call-done = bf16[1024,512]{0,1:T(8,128)(2,1)} async-done(((bf16[128,512]{0,1:T(8,128)(2,1)}), bf16[1024,512]{0,1:T(8,128)(2,1)}) %all-gather.2.cloned.1.call-update) | async-done | bytes 1048592 | tf_op jit(solution)/shard_map/all_gather | solution.py:54
  35.6 8.1 %fusion.2 = (f32[4,8,128]{2,1,0:T(8,128)S(1)}, f32[4,1024,128,8]{2,1,3,0:T(8,128)}) fusion(pred[128,1024]{0,1:T(8,128)(4,1)S(1)} %iota_compare_fusion, bf16[128,4,8,64]{0,3,2,1:T(8,128)(2,1)S(1)} %bitcast.78, bf16[1024,4,2,64]{0,3,2,1:T(8,128)(2,1)} %bitcast.80), kind=kOutput, calls=%fused_computation.7 | convolution fusion | flops 549449728 | bytes 17973248 | tf_op jit(solution)/shard_map/tgrd,ngd->grtn/dot_general | solution.py:60
  43.6 0.1 broadcast_maximum_fusion
  43.7 9.3 %fusion = f32[4,8,128]{2,1,0:T(8,128)S(1)} fusion(f32[4,1024,128,8]{2,1,3,0:T(8,128)} %get-tuple-element.12, f32[4,8,128]{2,1,0:T(8,128)S(1)} %broadcast_maximum_fusion, pred[128,1024]{0,1:T(8,128)(4,1)S(1)} %iota_compare_fusion), kind=kLoop, calls=%fused_computation.5 | loop fusion | flops 16773120 | bytes 16941056 | tf_op jit(solution)/shard_map/reduce_sum | solution.py:71
  53.0 0.1 multiply_bitcast_fusion
  53.1 7.8 %divide_convert_fusion = bf16[128,4,8,64]{0,3,2,1:T(8,128)(2,1)S(1)} fusion(f32[4,1024,128,8]{2,1,3,0:T(8,128)} %get-tuple-element.12, f32[4,8,128]{2,1,0:T(8,128)S(1)} %broadcast_maximum_fusion, pred[128,1024]{0,1:T(8,128)(4,1)S(1)} %iota_compare_fusion, bf16[1024,4,2,64]{0,3,2,1:T(8,128)(2,1)S(1)} %bitcast.81, f32[128,4,8]{0,2,1:T(8,128)S(1)} %get-tuple-element.10, ...), kind=kOutput, calls=%fused_computation.22 | convolution fusion | flops 554434560 | bytes 18006016 | tf_op jit(solution)/shard_map/grtn,ngd->grtd/dot_general | solution.py:72
  60.9 7.1 %convolution_convert_fusion.1 = bf16[128,2880]{0,1:T(8,128)(2,1)} fusion(bf16[2048,2880]{0,1:T(8,128)(2,1)} %param.14, bf16[128,2048]{0,1:T(8,128)(2,1)S(1)} %bitcast.85), kind=kOutput, calls=%fused_computation.12 | convolution fusion | flops 1510318080 | bytes 13058048 | tf_op jit(solution)/shard_map/dot_general | solution.py:89
  68.0 0.0 reduce-scatter.4.cloned.1.call-start
  68.1 0.1 mul.93
  68.2 2.6 scatter_custom_fusion
  70.9 29.3 %all-reduce.3.cloned.1.call-done = bf16[128,2880]{0,1:T(8,128)(2,1)} async-done(((bf16[128,2880]{0,1:T(8,128)(2,1)}), bf16[128,2880]{0,1:T(8,128)(2,1)}) %all-reduce.3.cloned.1.call-update) | async-done | bytes 737296 | tf_op jit(solution)/shard_map/psum | solution.py:90
  100.2 2.6 convert_add_fusion
  102.8 1.6 multiply_convert_fusion
  104.4 0.3 copy.46
  104.7 0.1 concatenate.3.clone
  104.8 4.6 %gather_fusion = bf16[640,2880]{1,0:T(8,128)(2,1)} fusion(bf16[129,2880]{1,0:T(8,128)(2,1)S(1)} %concatenate.3.clone, s32[1024]{0:T(1024)S(1)} %pad_clamp_fusion.1), kind=kCustom, calls=%fused_computation | custom fusion | bytes 7375360 | tf_op jit(solution)/shard_map/gather | solution.py:95
  109.4 89.4 %all_to_all.10 = bf16[8,80,2880]{2,1,0:T(8,128)(2,1)S(1)} all-to-all(bf16[8,80,2880]{2,1,0:T(8,128)(2,1)} %bitcast.75), channel_id=1, replica_groups=mesh['groups'=2,'tok'=8,'head'=2,'pair'=1] {'tok'}, dimensions={0} | all-to-all | bytes 7372800 | tf_op jit(solution)/shard_map/all_to_all | solution.py:96
  198.8 9.5 %fusion.28 = f32[640,1440]{0,1:T(8,128)S(1)} fusion(bf16[640,2880]{1,0:T(8,128)(2,1)S(1)} %bitcast.77, bf16[2880,1440]{0,1:T(8,128)(2,1)} %bitcast.84), kind=kOutput, calls=%fused_computation.58 | convolution fusion | flops 5308416000 | bytes 15667200 | tf_op jit(solution)/shard_map/dot_general | solution.py:25
  208.3 0.5 fusion.8
  208.8 1.0 copy.37
  209.9 7.0 %convolution_convert_fusion = bf16[8,80,2880]{2,1,0:T(8,128)(2,1)} fusion(bf16[8,80,720]{2,1,0:T(8,128)(2,1)S(1)} %bitcast.79, bf16[1,720,2880]{2,1,0:T(8,128)(2,1)} %param.19), kind=kOutput, calls=%fused_computation.10 | convolution fusion | flops 2656051200 | bytes 8755200 | tf_op jit(solution)/shard_map/dot_general | solution.py:99
  216.9 8.1 %copy.42 = bf16[8,80,2880]{1,0,2:T(8,128)(2,1)} copy(bf16[8,80,2880]{2,1,0:T(8,128)(2,1)} %convolution_convert_fusion) | data formatting | bytes 7372800
  225.0 9.6 %reshape.137 = bf16[2880,640]{1,0:T(8,128)(2,1)} reshape(bf16[2880,8,80]{2,1,0:T(8,128)(2,1)} %bitcast.74) | data formatting | bytes 7372800
  234.6 47.5 %reduce-scatter.4.cloned.1.call-done = bf16[1440,640]{1,0:T(8,128)(2,1)} async-done(((bf16[2880,640]{1,0:T(8,128)(2,1)}), bf16[1440,640]{1,0:T(8,128)(2,1)}) %reduce-scatter.4.cloned.1.call-update) | async-done | bytes 1843216
  282.1 4.8 %reshape.138 = bf16[1440,8,80]{2,1,0:T(8,128)(2,1)S(1)} reshape(bf16[1440,640]{1,0:T(8,128)(2,1)} %reduce-scatter.4.cloned.1.call-done) | data formatting | bytes 3686400
  286.9 3.5 copy.43
  290.5 4.6 %all-to-all-start.1 = ((bf16[8,80,1440]{2,1,0:T(8,128)(2,1)}), bf16[8,80,1440]{2,1,0:T(8,128)(2,1)S(1)}, u32[]{:S(2)}, u32[]{:S(2)}) async-start(bf16[8,80,1440]{2,1,0:T(8,128)(2,1)} %copy.43), calls=%async_computation.1 | async-start | bytes 3932160 | tf_op jit(solution)/shard_map/all_to_all | solution.py:105
  295.1 0.1 reshape.116
  295.2 0.1 copy.32
  295.3 46.0 %all-to-all-done.1 = bf16[8,80,1440]{2,1,0:T(8,128)(2,1)S(1)} async-done(((bf16[8,80,1440]{2,1,0:T(8,128)(2,1)}), bf16[8,80,1440]{2,1,0:T(8,128)(2,1)S(1)}, u32[]{:S(2)}, u32[]{:S(2)}) %all-to-all-start.1) | async-done | bytes 1843232 | tf_op jit(solution)/shard_map/all_to_all | solution.py:105
  341.3 3.0 gather_fusion.1
  344.2 2.9 reshape.133
  347.2 3.1 multiply_reduce_fusion
  350.2 1.4 copy.38
  351.6 1.9 add_convert_fusion
  (22 shorter events, 0.2 us)
Async XLA Ops:
  6.5 29.0 %all-gather.2.cloned.1.call-start = ((), (), s32[]{:S(2)}) async-start(), calls=%async_computation.3 | async-start | bytes 1179648 | tf_op jit(solution)/shard_map/all_gather | solution.py:54
  8.2 92.0 %all-reduce.3.cloned.1.call-start = ((), (), s32[]{:S(2)}) async-start(), calls=%async_computation.4 | async-start | bytes 1474560 | tf_op jit(solution)/shard_map/psum | solution.py:90
  43.7 9.3 %copy-start.1 = (bf16[1024,512]{0,1:T(8,128)(2,1)S(1)}, bf16[1024,512]{0,1:T(8,128)(2,1)}, u32[]{:S(2)}) copy-start(bf16[1024,512]{0,1:T(8,128)(2,1)} %all-gather.2.cloned.1.call-done) | copy-start | bytes 3145732
  60.9 39.3 %copy-start = (bf16[128,2880]{0,1:T(8,128)(2,1)S(1)}, bf16[128,2880]{0,1:T(8,128)(2,1)}, u32[]{:S(2)}) copy-start(bf16[128,2880]{0,1:T(8,128)(2,1)} %param.13) | copy-start | bytes 2211844
  68.0 34.8 %copy-start.2 = (f32[2880]{0:T(1024)S(1)}, f32[2880]{0:T(1024)}, u32[]{:S(2)}) copy-start(f32[2880]{0:T(1024)} %param.15) | copy-start | bytes 34564
  68.0 214.1 %reduce-scatter.4.cloned.1.call-start = ((), (), s32[]{:S(2)}) async-start(), calls=%async_computation.5 | async-start | bytes 5529600
  286.9 8.3 %copy-start.3 = (f32[128,4]{0,1:T(4,128)S(1)}, f32[128,4]{0,1:T(4,128)}, u32[]{:S(2)}) copy-start(f32[128,4]{0,1:T(4,128)} %param.17) | copy-start | bytes 6148
  290.5 50.8 %all-to-all-start.1 = ((bf16[8,80,1440]{2,1,0:T(8,128)(2,1)}), bf16[8,80,1440]{2,1,0:T(8,128)(2,1)S(1)}, u32[]{:S(2)}, u32[]{:S(2)}) async-start(bf16[8,80,1440]{2,1,0:T(8,128)(2,1)} %copy.43), calls=%async_computation.1 | async-start | bytes 3932160 | tf_op jit(solution)/shard_map/all_to_all | solution.py:105
Sparse Core Ops, SparseCore 0:
  8.9 26.5 all-gather.1
  68.1 32.0 all-reduce.2
  234.7 47.3 reduce-scatter.3
where the time goes:
time: 361 us; the launch traced here: 360 us
  waiting for transfers between devices  145 us (40%)
  blocking collectives  89.4 us (25%)
  local copies, waits for them, and re-layouts  47.4 us (13%)
  matrix products  39.4 us (11%)
  other arithmetic  20.5 us (6%)
  between operations  13.3 us (4%)
  starting transfers between devices  4.69 us (1%)
    all_to_all x1, blocking collectives, per_device(): lax.all_to_all(outgoing, 'tok', split_axis=0, concat_axis=0, tiled=True)  89.4 us
    unnamed x4, waiting for transfers between devices  47.5 us
    all_to_all x1, waiting for transfers between devices, per_device(): lax.all_to_all(expert_out, 'tok', split_axis=0, concat_axis=0, tiled=True)  46 us
    unnamed x17, local copies, waits for them, and re-layouts  30.3 us
    psum x1, waiting for transfers between devices, per_device(): lax.psum(partial_value.astype(jnp.bfloat16), ('head', 'pair'))  29.3 us
    all_gather x1, waiting for transfers between devices, per_device(): key_piece = lax.all_gather(keys_values, 'tok', axis=0, tiled=True)  22.5 us
    dot_general x1, matrix products, active_rows(): both = jnp.dot(flat_rows, both_columns, preferred_element_type=jnp.float32)  9.46 us
    reduce_sum x1, other arithmetic, per_device(): totals = totals * decay + jnp.sum(weights, axis=-1)  9.26 us
  transfers between devices with their start and end apart: 4, of which 4 were waited for; matrix products, arithmetic and copies ran while one was open for 2% of the time, Pallas kernels for 0%

commit v1 on v0

--- a/solution.py
+++ b/solution.py
@@ -87,7 +87,9 @@
     share = width // lax.axis_size(("head", "pair"))
     column_start = lax.axis_index(("head", "pair")) * share
     partial_value = jnp.dot(attended, out_weight, preferred_element_type=jnp.float32)
-    projected = lax.psum(partial_value.astype(jnp.bfloat16), ("head", "pair")).astype(jnp.float32)
+    projected = jnp.sum(
+        lax.all_gather(partial_value.astype(jnp.bfloat16), ("head", "pair")), axis=0
+    ).astype(jnp.float32)
     stream = residual.astype(jnp.float32) + projected
     inverse = lax.rsqrt(jnp.mean(stream * stream, axis=-1, keepdims=True) + 1e-05)
     normed = (stream * inverse * norm_gain).astype(jnp.bfloat16)

time: 361 us -> 367 us (1.017)
  other arithmetic: 20.5 us -> 31 us
  waiting for transfers between devices: 145 us -> 138 us
    psum x1 -> x0, waiting for transfers between devices: 29.3 us -> none  [per_device(): lax.psum(partial_value.astype(jnp.bfloat16), ('head', 'pair'))]
    all_gather x0 -> x1, waiting for transfers between devices: none -> 19.8 us  [per_device(): lax.all_gather(partial_value.astype(jnp.bfloat16), ('head', 'pair'))]
    reduce_sum x0 -> x1, other arithmetic: none -> 15.3 us  [per_device(): jnp.sum(lax.all_gather(partial_value.astype(jnp.bfloat16), ('head', 'pair...]
    unnamed x17 -> x21, local copies, waits for them, and re-layouts: 30.3 us -> 29.6 us
where the time goes in v1:
time: 367 us; the launch traced here: 366 us
  waiting for transfers between devices  138 us (38%)
  blocking collectives  89.4 us (24%)
  local copies, waits for them, and re-layouts  49.8 us (14%)
  matrix products  39.5 us (11%)
  other arithmetic  31 us (8%)
  between operations  13.4 us (4%)
  starting transfers between devices  4.68 us (1%)
    all_to_all x1, blocking collectives, per_device(): lax.all_to_all(outgoing, 'tok', split_axis=0, concat_axis=0, tiled=True)  89.4 us
    unnamed x4, waiting for transfers between devices  47.6 us
    all_to_all x1, waiting for transfers between devices, per_device(): lax.all_to_all(expert_out, 'tok', split_axis=0, concat_axis=0, tiled=True)  46 us
    unnamed x21, local copies, waits for them, and re-layouts  29.6 us
    all_gather x1, waiting for transfers between devices, per_device(): key_piece = lax.all_gather(keys_values, 'tok', axis=0, tiled=True)  25.1 us
    all_gather x1, waiting for transfers between devices, per_device(): lax.all_gather(partial_value.astype(jnp.bfloat16), ('head', 'pair'))  19.8 us
    reduce_sum x1, other arithmetic, per_device(): jnp.sum(lax.all_gather(partial_value.astype(jnp.bfloat16), ('head', 'pair...  15.3 us
    dot_general x1, matrix products, active_rows(): both = jnp.dot(flat_rows, both_columns, preferred_element_type=jnp.float32)  9.44 us
  transfers between devices with their start and end apart: 4, of which 4 were waited for; matrix products, arithmetic and copies ran while one was open for 2% of the time, Pallas kernels for 0%

profile of v1, /device:TPU:0, one launch (start us, length us, event | category | flops | bytes accessed | tf_op | source)
XLA Modules:
  0.0 366.2 jit_solution(17279860285508581211)
XLA Ops:
  6.5 1.7 copy.30
  8.3 1.3 copy.32
  9.6 0.7 broadcast_in_dim.20
  10.3 0.1 iota_compare_fusion
  10.4 25.1 %all-gather.4.cloned.1.call-done = bf16[1024,512]{0,1:T(8,128)(2,1)} async-done(((bf16[128,512]{0,1:T(8,128)(2,1)}), bf16[1024,512]{0,1:T(8,128)(2,1)}) %all-gather.4.cloned.1.call-update) | async-done | bytes 1048592 | tf_op jit(solution)/shard_map/all_gather | solution.py:54
  35.6 8.1 %fusion.2 = (f32[4,8,128]{2,1,0:T(8,128)S(1)}, f32[4,1024,128,8]{2,1,3,0:T(8,128)}) fusion(pred[128,1024]{0,1:T(8,128)(4,1)S(1)} %iota_compare_fusion, bf16[128,4,8,64]{0,3,2,1:T(8,128)(2,1)S(1)} %bitcast.80, bf16[1024,4,2,64]{0,3,2,1:T(8,128)(2,1)} %bitcast.82), kind=kOutput, calls=%fused_computation.7 | convolution fusion | flops 549449728 | bytes 17973248 | tf_op jit(solution)/shard_map/tgrd,ngd->grtn/dot_general | solution.py:60
  43.6 0.1 broadcast_maximum_fusion
  43.7 9.4 %fusion = f32[4,8,128]{2,1,0:T(8,128)S(1)} fusion(f32[4,1024,128,8]{2,1,3,0:T(8,128)} %get-tuple-element.12, f32[4,8,128]{2,1,0:T(8,128)S(1)} %broadcast_maximum_fusion, pred[128,1024]{0,1:T(8,128)(4,1)S(1)} %iota_compare_fusion), kind=kLoop, calls=%fused_computation.5 | loop fusion | flops 16773120 | bytes 16941056 | tf_op jit(solution)/shard_map/reduce_sum | solution.py:71
  53.1 0.1 multiply_bitcast_fusion
  53.2 7.8 %divide_convert_fusion = bf16[128,4,8,64]{0,3,2,1:T(8,128)(2,1)S(1)} fusion(f32[4,1024,128,8]{2,1,3,0:T(8,128)} %get-tuple-element.12, f32[4,8,128]{2,1,0:T(8,128)S(1)} %broadcast_maximum_fusion, pred[128,1024]{0,1:T(8,128)(4,1)S(1)} %iota_compare_fusion, bf16[1024,4,2,64]{0,3,2,1:T(8,128)(2,1)S(1)} %bitcast.83, f32[128,4,8]{0,2,1:T(8,128)S(1)} %get-tuple-element.10, ...), kind=kOutput, calls=%fused_computation.22 | convolution fusion | flops 554434560 | bytes 18006016 | tf_op jit(solution)/shard_map/grtn,ngd->grtd/dot_general | solution.py:72
  61.1 7.1 %convolution_convert_fusion.1 = bf16[128,2880]{0,1:T(8,128)(2,1)} fusion(bf16[2048,2880]{0,1:T(8,128)(2,1)} %param.14, bf16[128,2048]{0,1:T(8,128)(2,1)S(1)} %bitcast.87), kind=kOutput, calls=%fused_computation.12 | convolution fusion | flops 1510318080 | bytes 13058048 | tf_op jit(solution)/shard_map/dot_general | solution.py:89
  68.3 0.1 copy.37
  68.4 0.1 eq.29
  68.5 0.1 eq.25
  68.6 0.3 copy.29
  69.0 1.1 reduce-window.6
  70.1 0.2 slice_reduce_fusion
  70.4 0.1 fusion.19
  70.5 0.1 reduce_sum.57
  70.6 0.1 mul.93
  70.7 2.6 scatter_custom_fusion
  73.4 19.8 %all-gather.6.cloned.1.call-done = bf16[256,2880]{0,1:T(8,128)(2,1)} async-done(((bf16[128,2880]{0,1:T(8,128)(2,1)}), bf16[256,2880]{0,1:T(8,128)(2,1)}) %all-gather.6.cloned.1.call-update) | async-done | bytes 1474576 | tf_op jit(solution)/shard_map/all_gather | solution.py:91
  93.2 3.2 reshape.130
  96.4 15.3 %reduce_sum.53 = bf16[128,2880]{0,1:T(8,128)(2,1)S(1)} reduce(bf16[2,128,2880]{1,0,2:T(2,128)(2,1)S(1)} %reshape.130, bf16[]{:T(256)} %constant.29.clone.1), dimensions={0}, to_apply=%region_2.3 | reduce | flops 368640 | bytes 2211842 | tf_op jit(solution)/shard_map/reduce_sum | solution.py:90
  111.7 0.3 copy.35
  112.0 1.4 convert_add_fusion
  113.4 0.3 multiply_convert_fusion
  113.7 0.1 concatenate.3
  113.8 4.6 %gather_fusion = bf16[640,2880]{1,0:T(8,128)(2,1)} fusion(bf16[129,2880]{1,0:T(8,128)(2,1)S(1)} %concatenate.3, s32[1024]{0:T(1024)S(1)} %pad_clamp_fusion.1), kind=kCustom, calls=%fused_computation | custom fusion | bytes 7375360 | tf_op jit(solution)/shard_map/gather | solution.py:97
  118.4 89.4 %all_to_all.10 = bf16[8,80,2880]{2,1,0:T(8,128)(2,1)S(1)} all-to-all(bf16[8,80,2880]{2,1,0:T(8,128)(2,1)} %bitcast.77), channel_id=1, replica_groups=mesh['groups'=2,'tok'=8,'head'=2,'pair'=1] {'tok'}, dimensions={0} | all-to-all | bytes 7372800 | tf_op jit(solution)/shard_map/all_to_all | solution.py:98
  207.8 9.4 %fusion.28 = f32[640,1440]{0,1:T(8,128)S(1)} fusion(bf16[640,2880]{1,0:T(8,128)(2,1)S(1)} %bitcast.79, bf16[2880,1440]{0,1:T(8,128)(2,1)} %bitcast.86), kind=kOutput, calls=%fused_computation.58 | convolution fusion | flops 5308416000 | bytes 15667200 | tf_op jit(solution)/shard_map/dot_general | solution.py:25
  217.3 0.5 fusion.8
  217.8 1.0 copy.40
  218.8 7.0 %convolution_convert_fusion = bf16[8,80,2880]{2,1,0:T(8,128)(2,1)} fusion(bf16[8,80,720]{2,1,0:T(8,128)(2,1)S(1)} %bitcast.81, bf16[1,720,2880]{2,1,0:T(8,128)(2,1)} %param.19), kind=kOutput, calls=%fused_computation.10 | convolution fusion | flops 2656051200 | bytes 8755200 | tf_op jit(solution)/shard_map/dot_general | solution.py:101
  225.8 8.1 %copy.45 = bf16[8,80,2880]{1,0,2:T(8,128)(2,1)} copy(bf16[8,80,2880]{2,1,0:T(8,128)(2,1)} %convolution_convert_fusion) | data formatting | bytes 7372800
  234.0 9.6 %reshape.138 = bf16[2880,640]{1,0:T(8,128)(2,1)} reshape(bf16[2880,8,80]{2,1,0:T(8,128)(2,1)} %bitcast.76) | data formatting | bytes 7372800
  243.6 47.5 %reduce-scatter.4.cloned.1.call-done = bf16[1440,640]{1,0:T(8,128)(2,1)} async-done(((bf16[2880,640]{1,0:T(8,128)(2,1)}), bf16[1440,640]{1,0:T(8,128)(2,1)}) %reduce-scatter.4.cloned.1.call-update) | async-done | bytes 1843216
  291.1 4.8 %reshape.139 = bf16[1440,8,80]{2,1,0:T(8,128)(2,1)S(1)} reshape(bf16[1440,640]{1,0:T(8,128)(2,1)} %reduce-scatter.4.cloned.1.call-done) | data formatting | bytes 3686400
  295.9 3.5 copy.46
  299.5 4.6 %all-to-all-start.1 = ((bf16[8,80,1440]{2,1,0:T(8,128)(2,1)}), bf16[8,80,1440]{2,1,0:T(8,128)(2,1)S(1)}, u32[]{:S(2)}, u32[]{:S(2)}) async-start(bf16[8,80,1440]{2,1,0:T(8,128)(2,1)} %copy.46), calls=%async_computation.1 | async-start | bytes 3932160 | tf_op jit(solution)/shard_map/all_to_all | solution.py:107
  304.1 0.1 reshape.116
  304.2 0.1 copy.36
  304.3 46.0 %all-to-all-done.1 = bf16[8,80,1440]{2,1,0:T(8,128)(2,1)S(1)} async-done(((bf16[8,80,1440]{2,1,0:T(8,128)(2,1)}), bf16[8,80,1440]{2,1,0:T(8,128)(2,1)S(1)}, u32[]{:S(2)}, u32[]{:S(2)}) %all-to-all-start.1) | async-done | bytes 1843232 | tf_op jit(solution)/shard_map/all_to_all | solution.py:107
  350.3 3.0 gather_fusion.1
  353.2 2.9 reshape.134
  356.2 2.2 multiply_reduce_fusion
  358.4 0.3 add_convert_fusion
  358.7 0.9 copy.41
  (29 shorter events, 0.3 us)
Async XLA Ops:
  6.5 29.0 %all-gather.4.cloned.1.call-start = ((), (), s32[]{:S(2)}) async-start(), calls=%async_computation.3 | async-start | bytes 1179648 | tf_op jit(solution)/shard_map/all_gather | solution.py:54
  8.2 84.9 %all-gather.6.cloned.1.call-start = ((), (), s32[]{:S(2)}) async-start(), calls=%async_computation.4 | async-start | bytes 2211840 | tf_op jit(solution)/shard_map/all_gather | solution.py:91
  43.7 9.5 %copy-start.2 = (bf16[1024,512]{0,1:T(8,128)(2,1)S(1)}, bf16[1024,512]{0,1:T(8,128)(2,1)}, u32[]{:S(2)}) copy-start(bf16[1024,512]{0,1:T(8,128)(2,1)} %all-gather.4.cloned.1.call-done) | copy-start | bytes 3145732
  61.0 7.2 %copy-start.4 = (s32[128,4]{0,1:T(4,128)S(1)}, s32[128,4]{0,1:T(4,128)}, u32[]{:S(2)}) copy-start(s32[128,4]{0,1:T(4,128)} %param.16) | copy-start | bytes 6148
  61.0 7.5 %copy-start.1 = (bf16[128,2880]{0,1:T(8,128)(2,1)S(1)}, bf16[128,2880]{0,1:T(8,128)(2,1)}, u32[]{:S(2)}) copy-start(bf16[128,2880]{0,1:T(8,128)(2,1)} %param.13) | copy-start | bytes 2211844
  68.2 222.9 %reduce-scatter.4.cloned.1.call-start = ((), (), s32[]{:S(2)}) async-start(), calls=%async_computation.5 | async-start | bytes 5529600
  96.4 17.1 %copy-start.3 = (f32[2880]{0:T(1024)S(1)}, f32[2880]{0:T(1024)}, u32[]{:S(2)}) copy-start(f32[2880]{0:T(1024)} %param.15) | copy-start | bytes 34564
  295.9 8.3 %copy-start.5 = (f32[128,4]{0,1:T(4,128)S(1)}, f32[128,4]{0,1:T(4,128)}, u32[]{:S(2)}) copy-start(f32[128,4]{0,1:T(4,128)} %param.17) | copy-start | bytes 6148
  299.5 50.8 %all-to-all-start.1 = ((bf16[8,80,1440]{2,1,0:T(8,128)(2,1)}), bf16[8,80,1440]{2,1,0:T(8,128)(2,1)S(1)}, u32[]{:S(2)}, u32[]{:S(2)}) async-start(bf16[8,80,1440]{2,1,0:T(8,128)(2,1)} %copy.46), calls=%async_computation.1 | async-start | bytes 3932160 | tf_op jit(solution)/shard_map/all_to_all | solution.py:107
  356.1 2.3 copy-start
Sparse Core Ops, SparseCore 0:
  8.9 26.5 all-gather.3
  68.3 24.8 all-gather.5
  243.7 47.3 reduce-scatter.3
